TPU v7x, 32 devices: a whole 2x2x4 slice. The times are simulated.
32 devices in a mesh: shard: 8 (over z, y), tp: 4 (over x, core).
Axes of the slice: x: 2, y: 2, z: 4, core: 2. Of those that a mesh axis runs over, the one named last changes fastest.
Arguments:
- weight_query: bfloat16 [12288, 12288], P('shard', 'tp'), may hold values from -0.078125 to 0.078125
- low_query: bfloat16 [12288, 64], P('shard'), may hold values from -0.0546875 to 0.0546875
- high_query: bfloat16 [64, 12288], P(None, 'tp'), may hold values from -0.75 to 0.75
- weight_key: bfloat16 [12288, 12288], P('shard', 'tp'), may hold values from -0.078125 to 0.078125
- low_key: bfloat16 [12288, 64], P('shard'), may hold values from -0.0546875 to 0.0546875
- high_key: bfloat16 [64, 12288], P(None, 'tp'), may hold values from -0.75 to 0.75
- weight_value: bfloat16 [12288, 12288], P('shard', 'tp'), may hold values from -0.078125 to 0.078125
- low_value: bfloat16 [12288, 64], P('shard'), may hold values from -0.0546875 to 0.0546875
- high_value: bfloat16 [64, 12288], P(None, 'tp'), may hold values from -0.75 to 0.75
- norm_train: float32 [12288], P(('shard', 'tp')), may hold values from 0.25 to 1.75
- norm_step: float32 [12288], P(('shard', 'tp')), may hold values from -0.3 to 0.3
Outputs:
- ready_query: bfloat16 [12288, 12288], P(None, ('tp', 'shard'))
- ready_key: bfloat16 [12288, 12288], P(None, ('tp', 'shard'))
- ready_value: bfloat16 [12288, 12288], P(None, ('tp', 'shard'))
- column_query: float32 [12288], P(('tp', 'shard'))
- column_key: float32 [12288], P(('tp', 'shard'))
- column_value: float32 [12288], P(('tp', 'shard'))
- serve_norm: bfloat16 [12288], replicated
All inputs are finite; a program needn't handle non-finite values. Where the computation divides by a largest or mean magnitude, that divisor is 1e-20 or more.
Results may differ from a plain program's by a relative error of at most 0.001.
Values may be sent and summed in bfloat16 or wider, within the bound.
A program may use at most 192 MiB of HBM per device.

v0:
```python
import jax
import jax.numpy as jnp
from jax import lax
from jax.sharding import PartitionSpec as P

D_MODEL = 12288


mix_rate = 0.5


def body(
    weight_query,
    low_query,
    high_query,
    weight_key,
    low_key,
    high_key,
    weight_value,
    low_value,
    high_value,
    norm_train,
    norm_step,
):
    latest_query = weight_query.astype(jnp.float32) + mix_rate * jnp.dot(
        low_query, high_query, preferred_element_type=jnp.float32
    )
    latest_key = weight_key.astype(jnp.float32) + mix_rate * jnp.dot(
        low_key, high_key, preferred_element_type=jnp.float32
    )
    latest_value = weight_value.astype(jnp.float32) + mix_rate * jnp.dot(
        low_value, high_value, preferred_element_type=jnp.float32
    )
    total_query, total_key, total_value = lax.psum(
        (
            jnp.sum(jnp.abs(latest_query), axis=0),
            jnp.sum(jnp.abs(latest_key), axis=0),
            jnp.sum(jnp.abs(latest_value), axis=0),
        ),
        "shard",
    )
    column_query = total_query / D_MODEL
    column_key = total_key / D_MODEL
    column_value = total_value / D_MODEL
    narrow_query, narrow_key, narrow_value = (
        (latest_query / column_query).astype(jnp.bfloat16),
        (latest_key / column_key).astype(jnp.bfloat16),
        (latest_value / column_value).astype(jnp.bfloat16),
    )
    ready_query, ready_key, ready_value = (
        lax.all_to_all(narrow_query, "shard", split_axis=1, concat_axis=0, tiled=True),
        lax.all_to_all(narrow_key, "shard", split_axis=1, concat_axis=0, tiled=True),
        lax.all_to_all(narrow_value, "shard", split_axis=1, concat_axis=0, tiled=True),
    )
    place = lax.axis_index("shard")
    column_query = lax.dynamic_slice_in_dim(
        column_query, place * ready_query.shape[1], ready_query.shape[1]
    )
    column_key = lax.dynamic_slice_in_dim(
        column_key, place * ready_key.shape[1], ready_key.shape[1]
    )
    column_value = lax.dynamic_slice_in_dim(
        column_value, place * ready_value.shape[1], ready_value.shape[1]
    )
    serve_norm = lax.all_gather(
        (norm_train + norm_step).astype(jnp.bfloat16), ("shard", "tp"), axis=0, tiled=True
    )
    return (ready_query, ready_key, ready_value, column_query, column_key, column_value, serve_norm)


def solution(mesh):
    placed = (
        P("shard", "tp"),
        P("shard", None),
        P(None, "tp"),
        P("shard", "tp"),
        P("shard", None),
        P(None, "tp"),
        P("shard", "tp"),
        P("shard", None),
        P(None, "tp"),
        P(("shard", "tp")),
        P(("shard", "tp")),
    )
    return jax.shard_map(
        body,
        mesh=mesh,
        in_specs=placed,
        out_specs=(
            P(None, ("tp", "shard")),
            P(None, ("tp", "shard")),
            P(None, ("tp", "shard")),
            P(("tp", "shard")),
            P(("tp", "shard")),
            P(("tp", "shard")),
            P(),
        ),
        check_vma=False,
    )
```

profile of v0, /device:TPU:17, one launch (start us, length us, event | category | flops | bytes accessed | tf_op | source)
XLA Modules:
  0.0 766.1 jit_solution(11815559867222424857)
XLA Ops:
  0.6 0.0 copy-start
  0.7 0.0 copy-start.3
  0.7 1.0 copy-done
  1.6 13.8 %abs_reduce_fusion.2 = (f32[3072]{0:T(1024)S(1)}, f32[1536,3072]{1,0:T(8,128)}) fusion(bf16[1536,64]{0,1:T(8,128)(2,1)} %param.12, bf16[64,3072]{1,0:T(8,128)(2,1)S(1)} %copy-done, bf16[1536,3072]{1,0:T(8,128)(2,1)} %param.11), kind=kOutput, calls=%fused_computation.7 | convolution fusion | flops 627569664 | bytes 28913664 | tf_op jit(solution)/shard_map/dot_general | solution.py:25
  15.4 0.0 slice-start.2
  15.4 0.0 copy-start.4
  15.4 0.0 copy-start.6
  15.4 8.2 %abs_reduce_fusion.1 = (f32[3072]{0:T(1024)S(1)}, f32[1536,3072]{1,0:T(8,128)}) fusion(bf16[1536,64]{0,1:T(8,128)(2,1)S(1)} %copy-done.3, bf16[64,3072]{1,0:T(8,128)(2,1)S(1)} %copy-done.5, bf16[1536,3072]{1,0:T(8,128)(2,1)S(1)} %copy-done.2), kind=kOutput, calls=%fused_computation.4 | convolution fusion | flops 627569664 | bytes 28913664 | tf_op jit(solution)/shard_map/dot_general | solution.py:28
  23.7 8.2 %abs_reduce_fusion = (f32[3072]{0:T(1024)S(1)}, f32[1536,3072]{1,0:T(8,128)}) fusion(bf16[1536,64]{0,1:T(8,128)(2,1)S(1)} %copy-done.4, bf16[64,3072]{1,0:T(8,128)(2,1)S(1)} %copy-done.6, bf16[1536,3072]{1,0:T(8,128)(2,1)S(1)} %bitcast.34), kind=kOutput, calls=%fused_computation.1 | convolution fusion | flops 627569664 | bytes 28913664 | tf_op jit(solution)/shard_map/dot_general | solution.py:31
  31.9 25.8 %all-reduce = (f32[3072]{0:T(1024)S(1)}, f32[3072]{0:T(1024)S(1)}, f32[3072]{0:T(1024)S(1)}) all-reduce(f32[3072]{0:T(1024)S(1)} %get-tuple-element.10, f32[3072]{0:T(1024)S(1)} %get-tuple-element.12, f32[3072]{0:T(1024)S(1)} %get-tuple-element.14), channel_id=1, replica_groups=mesh['shard'=8,'tp'=4] {'shard'}, use_global_device_ids=true, to_apply=%region_1.0 | all-reduce | flops 9216 | bytes 73728 | tf_op jit(solution)/shard_map/psum | solution.py:34
  57.7 11.5 %divide_convert_fusion.2 = bf16[1536,3072]{1,0:T(8,128)(2,1)} fusion(f32[1536,3072]{1,0:T(8,128)} %get-tuple-element.11, f32[3072]{0:T(1024)S(1)} %broadcast_multiply_fusion.2), kind=kLoop, calls=%fused_computation.6 | loop fusion | flops 9437184 | bytes 28323840 | tf_op jit(solution)/shard_map/convert_element_type | solution.py:46
  69.2 8.4 %copy.35 = bf16[192,8,8,384]{3,2,0,1:T(8,128)(2,1)} copy(bf16[192,8,8,384]{3,2,1,0:T(8,128)(2,1)} %bitcast.30) | data formatting | bytes 18874368 | tf_op jit(solution)/shard_map/all_to_all | solution.py:51
  77.7 9.7 %all-to-all-start = ((bf16[1536,8,384]{2,0,1:T(8,128)(2,1)}), bf16[1536,8,384]{2,0,1:T(8,128)(2,1)}, u32[]{:S(2)}, u32[]{:S(2)}) async-start(bf16[1536,8,384]{2,0,1:T(8,128)(2,1)} %bitcast.29), calls=%async_computation | async-start | bytes 18874368 | tf_op jit(solution)/shard_map/all_to_all | solution.py:51
  87.4 11.5 %divide_convert_fusion.1 = bf16[1536,3072]{1,0:T(8,128)(2,1)} fusion(f32[1536,3072]{1,0:T(8,128)} %get-tuple-element.13, f32[3072]{0:T(1024)S(1)} %broadcast_multiply_fusion.1), kind=kLoop, calls=%fused_computation.3 | loop fusion | flops 9437184 | bytes 28323840 | tf_op jit(solution)/shard_map/convert_element_type | solution.py:47
  99.0 8.4 %copy.34 = bf16[192,8,8,384]{3,2,0,1:T(8,128)(2,1)} copy(bf16[192,8,8,384]{3,2,1,0:T(8,128)(2,1)} %bitcast.31) | data formatting | bytes 18874368 | tf_op jit(solution)/shard_map/all_to_all | solution.py:52
  107.4 174.8 %all-to-all-done = bf16[1536,8,384]{2,0,1:T(8,128)(2,1)} async-done(((bf16[1536,8,384]{2,0,1:T(8,128)(2,1)}), bf16[1536,8,384]{2,0,1:T(8,128)(2,1)}, u32[]{:S(2)}, u32[]{:S(2)}) %all-to-all-start) | async-done | bytes 9437216 | tf_op jit(solution)/shard_map/all_to_all | solution.py:51
  282.2 14.6 %all-to-all-start.1 = ((bf16[1536,8,384]{2,0,1:T(8,128)(2,1)}), bf16[1536,8,384]{2,0,1:T(8,128)(2,1)}, u32[]{:S(2)}, u32[]{:S(2)}) async-start(bf16[1536,8,384]{2,0,1:T(8,128)(2,1)} %bitcast.28), calls=%async_computation.1 | async-start | bytes 18874368 | tf_op jit(solution)/shard_map/all_to_all | solution.py:52
  296.9 11.5 %divide_convert_fusion = bf16[1536,3072]{1,0:T(8,128)(2,1)} fusion(f32[1536,3072]{1,0:T(8,128)} %get-tuple-element.15, f32[3072]{0:T(1024)S(1)} %broadcast_multiply_fusion), kind=kLoop, calls=%fused_computation | loop fusion | flops 9437184 | bytes 28323840 | tf_op jit(solution)/shard_map/convert_element_type | solution.py:48
  308.4 8.5 %copy.33 = bf16[192,8,8,384]{3,2,0,1:T(8,128)(2,1)} copy(bf16[192,8,8,384]{3,2,1,0:T(8,128)(2,1)} %bitcast.32) | data formatting | bytes 18874368 | tf_op jit(solution)/shard_map/all_to_all | solution.py:53
  316.9 180.6 %all-to-all-done.1 = bf16[1536,8,384]{2,0,1:T(8,128)(2,1)} async-done(((bf16[1536,8,384]{2,0,1:T(8,128)(2,1)}), bf16[1536,8,384]{2,0,1:T(8,128)(2,1)}, u32[]{:S(2)}, u32[]{:S(2)}) %all-to-all-start.1) | async-done | bytes 9437216 | tf_op jit(solution)/shard_map/all_to_all | solution.py:52
  497.5 9.1 %all-to-all-start.2 = ((bf16[1536,8,384]{2,0,1:T(8,128)(2,1)}), bf16[1536,8,384]{2,0,1:T(8,128)(2,1)}, u32[]{:S(2)}, u32[]{:S(2)}) async-start(bf16[1536,8,384]{2,0,1:T(8,128)(2,1)} %bitcast.27), calls=%async_computation.2 | async-start | bytes 18874368 | tf_op jit(solution)/shard_map/all_to_all | solution.py:53
  506.5 0.7 dynamic_slice.9
  507.2 0.7 dynamic_slice.10
  507.8 0.7 dynamic_slice.11
  508.5 0.0 copy-done.7
  508.5 228.9 %all-gather = bf16[32,1,384]{2,1,0:T(2,128)(2,1)S(1)} all-gather(bf16[1,1,384]{2,1,0:T(2,128)(2,1)S(1)} %reshape.26), channel_id=1, replica_groups=mesh['shard'=8,'tp'=4] {'shard','tp'}, dimensions={0}, use_global_device_ids=true | all-gather | bytes 25344 | tf_op jit(solution)/shard_map/all_gather | solution.py:65
  737.4 0.1 reduce
  737.6 0.6 reshape.27
  738.2 0.0 all-to-all-done.2
  738.2 9.3 %copy.39 = bf16[12288,384]{1,0:T(8,128)(2,1)} copy(bf16[12288,384]{1,0:T(8,128)(2,1)} %bitcast.1) | data formatting | bytes 18874368
  747.5 9.3 %copy.40 = bf16[12288,384]{1,0:T(8,128)(2,1)} copy(bf16[12288,384]{1,0:T(8,128)(2,1)} %bitcast.3) | data formatting | bytes 18874368
  756.8 9.3 %copy.41 = bf16[12288,384]{1,0:T(8,128)(2,1)} copy(bf16[12288,384]{1,0:T(8,128)(2,1)} %bitcast.5) | data formatting | bytes 18874368
  (23 shorter events, 0.1 us)
Async XLA Ops:
  0.6 1.0 copy-start
  0.7 14.8 %copy-start.3 = (bf16[1536,64]{0,1:T(8,128)(2,1)S(1)}, bf16[1536,64]{0,1:T(8,128)(2,1)}, u32[]{:S(2)}) copy-start(bf16[1536,64]{0,1:T(8,128)(2,1)} %param.15) | copy-start | bytes 589828
  0.7 14.7 %copy-start.5 = (bf16[64,3072]{1,0:T(8,128)(2,1)S(1)}, bf16[64,3072]{1,0:T(8,128)(2,1)}, u32[]{:S(2)}) copy-start(bf16[64,3072]{1,0:T(8,128)(2,1)} %param.16) | copy-start | bytes 1179652
  0.7 14.7 %copy-start.2 = (bf16[1536,3072]{1,0:T(8,128)(2,1)S(1)}, bf16[1536,3072]{1,0:T(8,128)(2,1)}, u32[]{:S(2)}) copy-start(bf16[1536,3072]{1,0:T(8,128)(2,1)} %param.14) | copy-start | bytes 28311556
  1.6 22.1 %slice-start = ((s8[9437184]{0:T(1024)(128)(4,1)}), s8[4194304]{0:T(1024)(128)(4,1)S(1)}, s32[]{:S(2)}) async-start(s8[9437184]{0:T(1024)(128)(4,1)} %bitcast.33), calls=%async_computation.3 | async-start | bytes 8388608
  1.6 22.1 %slice-start.1 = ((s8[9437184]{0:T(1024)(128)(4,1)}), s8[4194304]{0:T(1024)(128)(4,1)S(1)}, s32[]{:S(2)}) async-start(s8[9437184]{0:T(1024)(128)(4,1)} %bitcast.33), calls=%async_computation.4 | async-start | bytes 8388608
  15.4 8.3 %slice-start.2 = ((s8[9437184]{0:T(1024)(128)(4,1)}), s8[1048576]{0:T(1024)(128)(4,1)S(1)}, s32[]{:S(2)}) async-start(s8[9437184]{0:T(1024)(128)(4,1)} %bitcast.33), calls=%async_computation.5 | async-start | bytes 2097152
  15.4 8.3 %copy-start.4 = (bf16[1536,64]{0,1:T(8,128)(2,1)S(1)}, bf16[1536,64]{0,1:T(8,128)(2,1)}, u32[]{:S(2)}) copy-start(bf16[1536,64]{0,1:T(8,128)(2,1)} %param.18) | copy-start | bytes 589828
  15.4 8.3 %copy-start.6 = (bf16[64,3072]{1,0:T(8,128)(2,1)S(1)}, bf16[64,3072]{1,0:T(8,128)(2,1)}, u32[]{:S(2)}) copy-start(bf16[64,3072]{1,0:T(8,128)(2,1)} %param.19) | copy-start | bytes 1179652
  77.7 204.6 %all-to-all-start = ((bf16[1536,8,384]{2,0,1:T(8,128)(2,1)}), bf16[1536,8,384]{2,0,1:T(8,128)(2,1)}, u32[]{:S(2)}, u32[]{:S(2)}) async-start(bf16[1536,8,384]{2,0,1:T(8,128)(2,1)} %bitcast.29), calls=%async_computation | async-start | bytes 18874368 | tf_op jit(solution)/shard_map/all_to_all | solution.py:51
  282.2 215.2 %all-to-all-start.1 = ((bf16[1536,8,384]{2,0,1:T(8,128)(2,1)}), bf16[1536,8,384]{2,0,1:T(8,128)(2,1)}, u32[]{:S(2)}, u32[]{:S(2)}) async-start(bf16[1536,8,384]{2,0,1:T(8,128)(2,1)} %bitcast.28), calls=%async_computation.1 | async-start | bytes 18874368 | tf_op jit(solution)/shard_map/all_to_all | solution.py:52
  308.4 200.1 %copy-start.7 = (f32[384]{0:T(512)S(1)}, f32[384]{0:T(512)}, u32[]{:S(2)}) copy-start(f32[384]{0:T(512)} %param.20) | copy-start | bytes 4612
  308.4 200.1 %copy-start.8 = (f32[384]{0:T(512)S(1)}, f32[384]{0:T(512)}, u32[]{:S(2)}) copy-start(f32[384]{0:T(512)} %param.21) | copy-start | bytes 4612
  497.5 240.7 %all-to-all-start.2 = ((bf16[1536,8,384]{2,0,1:T(8,128)(2,1)}), bf16[1536,8,384]{2,0,1:T(8,128)(2,1)}, u32[]{:S(2)}, u32[]{:S(2)}) async-start(bf16[1536,8,384]{2,0,1:T(8,128)(2,1)} %bitcast.27), calls=%async_computation.2 | async-start | bytes 18874368 | tf_op jit(solution)/shard_map/all_to_all | solution.py:53
  738.2 27.9 %copy-start.1 = (bf16[64,3072]{1,0:T(8,128)(2,1)S(1)}, bf16[64,3072]{1,0:T(8,128)(2,1)}, u32[]{:S(2)}) copy-start(bf16[64,3072]{1,0:T(8,128)(2,1)} %param.13) | copy-start | bytes 1179652
where the time goes:
time: 767 us; the launch traced here: 766 us
  waiting for transfers between devices  355 us (46%)
  blocking collectives  255 us (33%)
  local copies, waits for them, and re-layouts  56.9 us (7%)
  other arithmetic  34.7 us (5%)
  starting transfers between devices  33.4 us (4%)
  matrix products  30.2 us (4%)
    all_gather x1, blocking collectives, body(): lax.all_gather((norm_train + norm_step).astype(jnp.bfloat16), ('shard', '...  229 us
    all_to_all x1, waiting for transfers between devices, body(): lax.all_to_all(narrow_key, 'shard', split_axis=1, concat_axis=0, tiled=True)  181 us
    all_to_all x1, waiting for transfers between devices, body(): lax.all_to_all(narrow_query, 'shard', split_axis=1, concat_axis=0, tiled=...  175 us
    unnamed x29, local copies, waits for them, and re-layouts  29.5 us
    psum x1, blocking collectives, body(): lax.psum((jnp.sum(jnp.abs(latest_query), axis=0), jnp.sum(jnp.abs(latest_...  25.8 us
  transfers between devices with their start and end apart: 3, of which 2 were waited for; matrix products, arithmetic and copies ran while one was open for 6% of the time, Pallas kernels for 0%

commit v1 on v0

v1 whole, which is shorter than its diff:
```python
import functools

import jax
import jax.numpy as jnp
from jax import lax
from jax.experimental import pallas as pl
from jax.experimental.pallas import tpu as pltpu
from jax.sharding import PartitionSpec as P

mix_rate = 0.5
MESH = pl.DeviceIdType.MESH
TILE = 256
RAW = 128


def merged(weight, low, high):
    product = jnp.dot(low, high, preferred_element_type=jnp.float32)
    return weight.astype(jnp.float32) + mix_rate * product


def exchange(
    n, parts, depth,
    wq, wk, wv, lq, lk, lv, hq, hk, hv, train, step,
    land_q, land_k, land_v, col_out, norm_out,
    wbuf, ltbuf, lbuf, hbuf, stat, col, raw, rawlow, fin, norm,
    load_sem, high_sem, low_sem, own_sem, fin_sem,
    send_sem, recv_sem, stat_send, stat_recv, raw_send, raw_recv,
    rlow_send, rlow_recv, norm_send, norm_recv, side_send, side_recv,
):
    weights, lows, highs = (wq, wk, wv), (lq, lk, lv), (hq, hk, hv)
    lands = (land_q, land_k, land_v)
    rows, width = wbuf.shape[2], wbuf.shape[3]
    me, side = lax.axis_index("shard"), lax.axis_index("tp")
    half = n // 2
    top, low_place = me // half, me % half

    def target(k):
        return lax.rem(1 - top + k // half, 2) * half + lax.rem(low_place + k % half, half)

    def cols(k):
        return pl.ds(pl.multiple_of(target(k) * width, 128), width)

    order = list(range(n))
    others = [k for k in order if k != half]
    loads = {}
    for m in range(3):
        low_copy = pltpu.make_async_copy(lows[m], ltbuf.at[m], low_sem.at[m])
        low_copy.start()
        loads[m] = low_copy
        for k in order:
            loads[m, k] = (
                pltpu.make_async_copy(highs[m].at[:, cols(k)], hbuf.at[m, k], high_sem.at[m, k]),
                pltpu.make_async_copy(weights[m].at[:, cols(k)], wbuf.at[m, k], load_sem.at[m, k]),
            )
            for copy in loads[m, k]:
                copy.start()

    norm[side, me, 0, :] = train[...] + step[...]

    barrier = pltpu.get_barrier_semaphore()
    for k in others:
        pl.semaphore_signal(barrier, inc=1, device_id={"shard": target(k)}, device_id_type=MESH)
    for j in range(1, parts):
        pl.semaphore_signal(
            barrier, inc=1, device_id={"tp": lax.rem(side + j, parts)}, device_id_type=MESH
        )
    pl.semaphore_wait(barrier, n - 1 + parts - 1)

    def remote(src, dst, send, recv, device):
        copy = pltpu.make_async_remote_copy(
            src_ref=src, dst_ref=dst, send_sem=send, recv_sem=recv,
            device_id=device, device_id_type=MESH,
        )
        copy.start()
        return copy

    raws, raw_lows = [], []
    for k in range(half):
        there = {"shard": target(k)}
        raw_lows.append(remote(
            lv.at[:, pl.ds(0, RAW)], rawlow.at[k], rlow_send.at[k], rlow_recv.at[k], there
        ))
        raws.append(remote(
            wv.at[pl.ds(0, RAW), cols(k)], raw.at[k], raw_send.at[k], raw_recv.at[k], there
        ))
    norms = [
        remote(norm.at[side, me], norm.at[side, me], norm_send.at[k], norm_recv.at[k], {"shard": target(k)})
        for k in others
    ]

    def sums(m):
        loads[m].wait()
        lbuf[m] = jnp.transpose(ltbuf[m].astype(jnp.float32)).astype(jnp.bfloat16)
        for k in order:
            for copy in loads[m, k]:
                copy.wait()

            def tile(i, total):
                at = pl.ds(pl.multiple_of(i * TILE, TILE), TILE)
                latest = merged(wbuf[m, k, at, :], lbuf[m, at, :], hbuf[m, k])
                return total + jnp.sum(jnp.abs(latest), axis=0, keepdims=True)

            total = lax.fori_loop(0, rows // TILE, tile, jnp.zeros((1, width), jnp.float32))
            stat[m, me, pl.ds(target(k), 1), :] = total
        return [
            remote(stat.at[m, me], stat.at[m, me], stat_send.at[m, k], stat_recv.at[m, k], {"shard": target(k)})
            for k in others
        ]

    def columns(m, copies):
        for copy in copies:
            copy.wait()
        total = stat[m, 0]
        for s in range(1, n):
            total = total + stat[m, s]
        col[m] = total / depth
        col_out[m] = col[m, pl.ds(me, 1), :]

    sent, own = [], []

    def send(m, k):
        first = RAW if m == 2 and k < half else 0
        if k == half:
            copy = pltpu.make_async_copy(
                wbuf.at[m, k], lands[m].at[pl.ds(pl.multiple_of(me * rows, 16), rows)], own_sem.at[m]
            )
            copy.start()
            own.append(copy)
            return
        sent.append(remote(
            wbuf.at[m, k, pl.ds(first, rows - first)],
            lands[m].at[pl.ds(pl.multiple_of(me * rows + first, 16), rows - first)],
            send_sem.at[m, k], recv_sem.at[m, k], {"shard": target(k)},
        ))

    def ready(m, behind):
        for k in order:
            scale = col[m, pl.ds(target(k), 1), :]

            def tile(i, carry):
                at = pl.ds(pl.multiple_of(i * TILE, TILE), TILE)
                latest = merged(wbuf[m, k, at, :], lbuf[m, at, :], hbuf[m, k])
                wbuf[m, k, at, :] = (latest / scale).astype(jnp.bfloat16)
                return carry

            lax.fori_loop(0, rows // TILE, tile, 0)
            if behind is not None:
                send(*behind)
            behind = (m, k)
        return behind

    stats = [sums(0), sums(1)]
    columns(0, stats[0])
    behind = ready(0, None)
    stats.append(sums(2))
    columns(1, stats[1])
    behind = ready(1, behind)
    columns(2, stats[2])
    behind = ready(2, behind)
    send(*behind)

    for copy in norms:
        copy.wait()
    sides = [
        remote(norm.at[side], norm.at[side], side_send.at[j], side_recv.at[j], {"tp": lax.rem(side + j, parts)})
        for j in range(1, parts)
    ]

    scale = col[2, pl.ds(me, 1), :]
    fins = []
    for k in range(half):
        raw_lows[k].wait()
        raws[k].wait()
        low = jnp.transpose(rawlow[k].astype(jnp.float32)).astype(jnp.bfloat16)
        latest = merged(raw[k], low, hbuf[2, half])
        fin[k] = (latest / scale).astype(jnp.bfloat16)
        source = (1 - top) * half + lax.rem(low_place + half - k, half)
        copy = pltpu.make_async_copy(
            fin.at[k], land_v.at[pl.ds(pl.multiple_of(source * rows, 16), RAW)], fin_sem.at[k]
        )
        copy.start()
        fins.append(copy)

    for copy in sides:
        copy.wait()
    norm_out[...] = norm[...]
    for copy in fins + own + sent:
        copy.wait()


def copy_out(q_in, k_in, v_in, q_out, k_out, v_out):
    q_out[...] = q_in[...]
    k_out[...] = k_in[...]
    v_out[...] = v_in[...]


def kernel_body(
    n, parts,
    weight_query, low_query, high_query,
    weight_key, low_key, high_key,
    weight_value, low_value, high_value,
    norm_train, norm_step,
):
    rows, wide = weight_query.shape
    width, depth = wide // n, rows * n
    rank, piece = low_query.shape[1], norm_train.shape[0]
    anywhere = pl.BlockSpec(memory_space=pl.ANY)
    vmem = pl.BlockSpec(memory_space=pltpu.VMEM)
    land = jax.ShapeDtypeStruct((depth, width), jnp.bfloat16)
    dma = pltpu.SemaphoreType.DMA
    half = n // 2
    land_q, land_k, land_v, column, norm = pl.pallas_call(
        functools.partial(exchange, n, parts, depth),
        out_shape=(
            land, land, land,
            jax.ShapeDtypeStruct((3, 1, width), jnp.float32),
            jax.ShapeDtypeStruct((parts, n, 1, piece), jnp.float32),
        ),
        in_specs=[anywhere] * 9 + [vmem] * 2,
        out_specs=(anywhere, anywhere, anywhere, vmem, vmem),
        scratch_shapes=[
            pltpu.VMEM((3, n, rows, width), jnp.bfloat16),
            pltpu.VMEM((3, rank, rows), jnp.bfloat16),
            pltpu.VMEM((3, rows, rank), jnp.bfloat16),
            pltpu.VMEM((3, n, rank, width), jnp.bfloat16),
            pltpu.VMEM((3, n, n, width), jnp.float32),
            pltpu.VMEM((3, n, width), jnp.float32),
            pltpu.VMEM((half, RAW, width), jnp.bfloat16),
            pltpu.VMEM((half, rank, RAW), jnp.bfloat16),
            pltpu.VMEM((half, RAW, width), jnp.bfloat16),
            pltpu.VMEM((parts, n, 1, piece), jnp.float32),
            dma((3, n)), dma((3, n)), dma((3,)), dma((3,)), dma((half,)),
            dma((3, n)), dma((3, n)), dma((3, n)), dma((3, n)),
            dma((half,)), dma((half,)), dma((half,)), dma((half,)),
            dma((n,)), dma((n,)), dma((parts,)), dma((parts,)),
        ],
        compiler_params=pltpu.CompilerParams(
            collective_id=0, has_side_effects=True, vmem_limit_bytes=56 * 2**20
        ),
        name="exchange",
    )(
        weight_query, weight_key, weight_value,
        low_query.T, low_key.T, low_value.T,
        high_query, high_key, high_value,
        norm_train, norm_step,
    )
    steps = 8
    block = pl.BlockSpec((depth // steps, width), lambda i: (i, 0))
    outs = pl.pallas_call(
        copy_out,
        grid=(steps,),
        out_shape=(land, land, land),
        in_specs=[block] * 3,
        out_specs=(block,) * 3,
        compiler_params=pltpu.CompilerParams(vmem_limit_bytes=48 * 2**20),
        name="copy_out",
    )(land_q, land_k, land_v)
    serve = jnp.transpose(norm.reshape(parts, n, piece), (1, 0, 2)).reshape(-1)
    return (*outs, column[0, 0], column[1, 0], column[2, 0], serve.astype(jnp.bfloat16))


def plain_body(
    weight_query, low_query, high_query,
    weight_key, low_key, high_key,
    weight_value, low_value, high_value,
    norm_train, norm_step,
):
    n = lax.axis_size("shard")
    latest = [
        merged(weight, low, high)
        for weight, low, high in (
            (weight_query, low_query, high_query),
            (weight_key, low_key, high_key),
            (weight_value, low_value, high_value),
        )
    ]
    totals = lax.psum(tuple(jnp.sum(jnp.abs(x), axis=0) for x in latest), "shard")
    place = lax.axis_index("shard")
    readies, columns = [], []
    for x, total in zip(latest, totals):
        column = total / (x.shape[0] * n)
        narrow = (x / column).astype(jnp.bfloat16)
        ready = lax.all_to_all(narrow, "shard", split_axis=1, concat_axis=0, tiled=True)
        readies.append(ready)
        columns.append(lax.dynamic_slice_in_dim(column, place * ready.shape[1], ready.shape[1]))
    serve = (norm_train + norm_step).astype(jnp.bfloat16)
    serve = lax.all_gather(serve, ("shard", "tp"), tiled=True)
    return (*readies, *columns, serve)


def solution(mesh):
    n, parts = mesh.shape["shard"], mesh.shape["tp"]

    def body(*args):
        rows, wide = args[0].shape
        fits = (
            n % 2 == 0
            and wide % (n * 128) == 0
            and rows % TILE == 0
            and all(args[i].shape == args[0].shape for i in (3, 6))
            and 6 * rows * wide < 40 * 2**20
        )
        if fits:
            return kernel_body(n, parts, *args)
        return plain_body(*args)

    weight, low, high = P("shard", "tp"), P("shard", None), P(None, "tp")
    norm = P(("shard", "tp"))
    ready, column = P(None, ("tp", "shard")), P(("tp", "shard"))
    return jax.shard_map(
        body,
        mesh=mesh,
        in_specs=(weight, low, high) * 3 + (norm, norm),
        out_specs=(ready,) * 3 + (column,) * 3 + (P(),),
        check_vma=False,
    )
```

time: 767 us -> 660 us (0.86)
  Pallas kernels: 0 us -> 652 us
  waiting for transfers between devices: 355 us -> 0 us
  blocking collectives: 255 us -> 0 us
  local copies, waits for them, and re-layouts: 56.9 us -> 1.25 us
  other arithmetic: 34.7 us -> 0.04 us
  starting transfers between devices: 33.4 us -> 0 us
  matrix products: 30.2 us -> 0 us
    pallas_call x0 -> x2, Pallas kernels: none -> 652 us  [the longest x1 632 us: kernel_body(): pl.pallas_call(functools.partial(exchange, n, parts, depth), out_shape=(l...]
    all_to_all x3 -> x0, waiting for transfers between devices: 355 us -> none  [the longest x1 181 us: body(): lax.all_to_all(narrow_key, 'shard', split_axis=1, concat_axis=0, tiled=True)]
    all_gather x1 -> x0, blocking collectives: 229 us -> none  [body(): lax.all_gather((norm_train + norm_step).astype(jnp.bfloat16), ('shard', '...]
    convert_element_type x4 -> x1, other arithmetic: 34.6 us -> 0.04 us  [kernel_body(): serve.astype(jnp.bfloat16)]
    all_to_all x3 -> x0, starting transfers between devices: 33.4 us -> none  [the longest x1 14.6 us: body(): lax.all_to_all(narrow_key, 'shard', split_axis=1, concat_axis=0, tiled=True)]
    dot_general x3 -> x0, matrix products: 30.2 us -> none  [the longest x1 13.8 us: body(): jnp.dot(low_query, high_query, preferred_element_type=jnp.float32)]
    unnamed x29 -> x5, local copies, waits for them, and re-layouts: 29.5 us -> 0.02 us
    psum x1 -> x0, blocking collectives: 25.8 us -> none  [body(): lax.psum((jnp.sum(jnp.abs(latest_query), axis=0), jnp.sum(jnp.abs(latest_...]
  transfers between devices with their start and end apart: 3 -> 0, of which waited for: 2 -> 0; matrix products, arithmetic and copies ran while one was open for 6% -> 0% of each run, Pallas kernels for 0% -> 0%
where the time goes in v1:
time: 660 us; the launch traced here: 654 us
  Pallas kernels  652 us (99%)
    pallas_call x1, Pallas kernels, kernel_body(): pl.pallas_call(functools.partial(exchange, n, parts, depth), out_shape=(l...  632 us
    pallas_call x1, Pallas kernels, kernel_body(): pl.pallas_call(copy_out, grid=(steps,), out_shape=(land, land, land), in_...  20.1 us

profile of v1, /device:TPU:17, one launch (start us, length us, event | category | flops | bytes accessed | tf_op | source)
XLA Modules:
  0.0 653.6 jit_solution(2670060648075740879)
XLA Ops:
  0.6 631.5 %exchange.1 = (bf16[12288,384]{1,0:T(8,128)(2,1)}, bf16[12288,384]{1,0:T(8,128)(2,1)}, bf16[12288,384]{1,0:T(8,128)(2,1)}, f32[3,1,384]{2,1,0:T(1,128)}, f32[4,8,1,384]{3,2,1,0:T(1,128)}) custom-call(bf16[1536,3072]{1,0:T(8,128)(2,1)} %wq.1, bf16[1536,3072]{1,0:T(8,128)(2,1)} %wk.1, bf16[1536,3072]{1,0:T(8,128)(2,1)} %wv.1, bf16[64,1536]{1,0:T(8,128)(2,1)} %bitcast.8, ...), custom_call_target="tpu_custom_call" | custom-call | tf_op jit(solution)/shard_map/exchange/pallas_call | solution.py:212
  632.2 0.0 copy-start.1
  632.2 0.0 copy-start
  632.2 20.1 %copy_out.1 = (bf16[12288,384]{1,0:T(8,128)(2,1)}, bf16[12288,384]{1,0:T(8,128)(2,1)}, bf16[12288,384]{1,0:T(8,128)(2,1)}) custom-call(bf16[12288,384]{1,0:T(8,128)(2,1)} %get-tuple-element.15.q_in, bf16[12288,384]{1,0:T(8,128)(2,1)} %get-tuple-element.16.k_in, bf16[12288,384]{1,0:T(8,128)(2,1)} %get-tuple-element.17.v_in), custom_call_target="tpu_custom_call" | custom-call | tf_op jit(solution)/shard_map/copy_out/pallas_call | solution.py:249
  652.3 0.0 copy-done.1
  652.3 0.6 slice_reduce_fusion
  652.9 0.0 copy-done
  652.9 0.6 convert_element_type.15
  (3 shorter events, 0.1 us)
Async XLA Ops:
  632.2 20.1 %copy-start.1 = (f32[3,1,384]{2,1,0:T(1,128)S(1)}, f32[3,1,384]{2,1,0:T(1,128)}, u32[]{:S(2)}) copy-start(f32[3,1,384]{2,1,0:T(1,128)} %get-tuple-element.21) | copy-start | bytes 13828
  632.2 20.7 %copy-start = (f32[4,8,1,384]{3,2,1,0:T(1,128)S(1)}, f32[4,8,1,384]{3,2,1,0:T(1,128)}, u32[]{:S(2)}) copy-start(f32[4,8,1,384]{3,2,1,0:T(1,128)} %get-tuple-element.22) | copy-start | bytes 147460
